TPU v7x, 32 devices: a whole 2x2x4 slice. The times are simulated.
32 devices in a mesh: beam: 2 (over x), fft: 16 (over z, y, core).
Axes of the slice: x: 2, y: 2, z: 4, core: 2. Of those that a mesh axis runs over, the one named last changes fastest.
Arguments:
- baseband: bfloat16 [4, 33554432], P('beam', 'fft'), parts along dimension 0, may hold values from -6 to 6
- spectrum_in: bfloat16 [4, 4096, 8192], P('beam', 'fft'), parts along dimension 0, may hold values from -6 to 6
- dm_index: int32 [1], replicated, may hold values from 0 to 63
Outputs:
- spectrum_out: bfloat16 [4, 4096, 8192], P('beam', 'fft'), parts along dimension 0
- smoothed: float32 [2, 2097152], P('beam', 'fft'), parts along dimension 0
There are 2 independent parts, one for each index of `beam`. A program takes and returns all parts, laid end to end along the dimension named above; an argument that names none is the same for every part. Nothing has to cross between parts.
Inputs may be any that keep to these rules, and one draw needn't show every extreme that they name: `dm_index`: indices into the grid of 64 trial dispersion measures.
All inputs are finite; a program needn't handle non-finite values.
Results may differ from a plain program's by a relative error of at most 0.0019.
The roundings to bfloat16 on the way count: a program that leaves them out, or rounds other values in their place, can miss the bound.
Values may be sent and summed in bfloat16 or wider, within the bound.
A program may use at most 128 MiB of HBM per device.

v0:
```python
import math

import jax
import jax.numpy as jnp
from jax import lax
from jax.sharding import PartitionSpec as P

ROWS_OUTER = 32
ROWS_INNER = 128
COLS_OUTER = 64
COLS_INNER = 128
ROW_LENGTH = 4096
COLUMN_LENGTH = 8192
SEGMENT_SAMPLES = 33554432
DM_GRID = 64
DECIMATE_FACTOR = 16
HALF_WIDTH = 16


def padded_2(block, sides, width):
    for axis, dim in sides:
        count = lax.axis_size(axis)
        forward = [(i, i + 1) for i in range(count - 1)]
        backward = [(target, source) for source, target in forward]
        low = lax.ppermute(
            lax.slice_in_dim(block, block.shape[dim] - width, None, axis=dim), axis, forward
        )
        high = lax.ppermute(lax.slice_in_dim(block, 0, width, axis=dim), axis, backward)
        block = jnp.concatenate([low, block, high], axis=dim)
    return block


def dft_table(length, direction):
    positions = jnp.arange(length, dtype=jnp.int32)
    product = jnp.remainder(positions[:, None] * positions[None, :], length)
    radians = direction * 2.0 * math.pi / length * product.astype(jnp.float32)
    norm_scale = 1.0 / math.sqrt(length)
    cosine = jnp.cos(radians) * norm_scale
    sine_part = jnp.sin(radians) * norm_scale
    return jnp.stack([jnp.stack([cosine, sine_part]), jnp.stack([-sine_part, cosine])]).astype(
        jnp.bfloat16
    )


def radians_of(numer, modulus, direction):
    return direction * 2.0 * math.pi / modulus * jnp.remainder(numer, modulus).astype(jnp.float32)


def chirp_radians(freq_row, col_outer, col_inner, grid_steps):
    col_freq = col_outer + COLS_OUTER * col_inner
    whole_mod = 4.0 * DM_GRID * ROW_LENGTH * COLUMN_LENGTH
    cross_mod = 2 * DM_GRID * COLUMN_LENGTH
    square_mod = 4 * DM_GRID * COLUMN_LENGTH
    grid_float = grid_steps.astype(jnp.float32)
    row_square = (freq_row * freq_row).astype(jnp.float32)
    term_rows = grid_float[:, None, None, None] * row_square[None, :, None, None] / whole_mod
    cross = jnp.remainder(freq_row[:, None, None] * col_freq[None], cross_mod)
    cross = jnp.remainder(grid_steps[:, None, None, None] * cross[None], cross_mod)
    square = jnp.remainder(col_freq * col_freq, square_mod)
    square = jnp.remainder(grid_steps[:, None, None] * square[None], square_mod)
    high_part = square // 512
    low_part = square % 512
    square = jnp.remainder(
        jnp.remainder(ROW_LENGTH * high_part, square_mod) * 512 + ROW_LENGTH * low_part, square_mod
    )
    turns = (
        term_rows
        + cross.astype(jnp.float32) / cross_mod
        + square[:, None].astype(jnp.float32) / square_mod
    )
    return 2.0 * math.pi * turns


def rotate(values, radians):
    cosine = jnp.cos(radians)
    sine_part = jnp.sin(radians)
    real_part = values[:, 0] * cosine - values[:, 1] * sine_part
    imag_part = values[:, 0] * sine_part + values[:, 1] * cosine
    return jnp.stack([real_part, imag_part], axis=1).astype(jnp.bfloat16)


def dft_section(values, einsum_form, length, direction, radians):
    mixed_sum = jnp.einsum(
        einsum_form, values, dft_table(length, direction), preferred_element_type=jnp.float32
    )
    if radians is None:
        return mixed_sum.astype(jnp.bfloat16)
    return rotate(mixed_sum, radians)


def row_frequency(row_pos):
    return row_pos // ROWS_INNER + ROWS_OUTER * (row_pos % ROWS_INNER)


def chirp_front(spectrum, grid_steps, row_start, row_local):
    trial_total = grid_steps.shape[0]
    row_pos = row_start + jnp.arange(row_local, dtype=jnp.int32)
    freq_row = row_frequency(row_pos)
    col_outer = jnp.arange(COLS_OUTER, dtype=jnp.int32)[:, None]
    col_inner = jnp.arange(COLS_INNER, dtype=jnp.int32)[None, :]
    values = rotate(
        spectrum.astype(jnp.float32).reshape(1, 2, row_local, COLS_OUTER, COLS_INNER),
        chirp_radians(freq_row, col_outer, col_inner, grid_steps),
    )
    values = dft_section(
        values,
        "dimjq,ioqy->domjy",
        COLS_INNER,
        1,
        radians_of(col_outer * col_inner, COLUMN_LENGTH, 1),
    )
    col_time = COLS_INNER * col_outer + col_inner
    values = dft_section(
        values,
        "dimjy,iojx->domxy",
        COLS_OUTER,
        1,
        radians_of(freq_row[:, None, None] * col_time[None], SEGMENT_SAMPLES, 1),
    )
    return values.reshape(trial_total, 2, row_local, COLUMN_LENGTH)


def finish_rows(values):
    trial_total = values.shape[0]
    col_local = values.shape[3]
    values = values.reshape(trial_total, 2, ROWS_OUTER, ROWS_INNER, col_local)
    outer_pos = jnp.arange(ROWS_OUTER, dtype=jnp.int32)[:, None]
    inner_pos = jnp.arange(ROWS_INNER, dtype=jnp.int32)[None, :]
    values = dft_section(
        values,
        "dikqb,ioqy->dokyb",
        ROWS_INNER,
        1,
        radians_of(outer_pos * inner_pos, ROW_LENGTH, 1)[:, :, None],
    )
    values = dft_section(values, "dikyb,iokx->doxyb", ROWS_OUTER, 1, None)
    return values.reshape(trial_total, 2, ROW_LENGTH, col_local)


def detect(values):
    trial_total = values.shape[0]
    row_total = values.shape[2]
    column_total = values.shape[3]
    wide = values.astype(jnp.float32)
    detected_power = wide[:, 0] * wide[:, 0] + wide[:, 1] * wide[:, 1]
    return jnp.mean(
        detected_power.reshape(
            trial_total, row_total, column_total // DECIMATE_FACTOR, DECIMATE_FACTOR
        ),
        axis=3,
    )


def on_device(baseband, spectrum_in, dm_index):
    device_index = lax.axis_index("fft")
    row_local = spectrum_in.shape[1]
    col_local = COLUMN_LENGTH // (ROW_LENGTH // row_local)
    values = baseband.reshape(2, row_local, COLUMN_LENGTH)
    values = lax.all_to_all(values, "fft", split_axis=2, concat_axis=1, tiled=True)
    values = values.reshape(1, 2, ROWS_OUTER, ROWS_INNER, col_local)
    outer_pos = jnp.arange(ROWS_OUTER, dtype=jnp.int32)[:, None]
    inner_pos = jnp.arange(ROWS_INNER, dtype=jnp.int32)[None, :]
    values = dft_section(
        values,
        "dixyb,ioxk->dokyb",
        ROWS_OUTER,
        -1,
        radians_of(outer_pos * inner_pos, ROW_LENGTH, -1)[:, :, None],
    )
    freq_row = outer_pos + ROWS_OUTER * inner_pos
    col_pos = device_index * col_local + jnp.arange(col_local, dtype=jnp.int32)
    values = dft_section(
        values,
        "dikyb,ioyq->dokqb",
        ROWS_INNER,
        -1,
        radians_of(freq_row[:, :, None] * col_pos[None, None, :], SEGMENT_SAMPLES, -1),
    )
    values = values.reshape(1, 2, ROW_LENGTH, col_local)
    values = lax.all_to_all(values, "fft", split_axis=2, concat_axis=3, tiled=True)
    values = values.reshape(1, 2, row_local, COLS_OUTER, COLS_INNER)
    col_outer = jnp.arange(COLS_OUTER, dtype=jnp.int32)[:, None]
    col_inner = jnp.arange(COLS_INNER, dtype=jnp.int32)[None, :]
    values = dft_section(
        values,
        "dimxy,ioxj->domjy",
        COLS_OUTER,
        -1,
        radians_of(col_outer * col_inner, COLUMN_LENGTH, -1),
    )
    values = dft_section(values, "dimjy,ioyq->domjq", COLS_INNER, -1, None)
    spectrum_out = values[0].reshape(2, row_local, COLUMN_LENGTH)
    grid_steps = dm_index + 1
    row_start = device_index * row_local
    trial_total = dm_index.shape[0]
    front_part = chirp_front(spectrum_in, grid_steps, row_start, row_local)
    moved = lax.all_to_all(front_part, "fft", split_axis=3, concat_axis=2, tiled=True)
    pieces = finish_rows(moved)
    decimated_power = lax.all_to_all(
        detect(pieces).astype(jnp.bfloat16), "fft", split_axis=1, concat_axis=2, tiled=True
    ).astype(jnp.float32)
    series = decimated_power.reshape(
        trial_total, decimated_power.shape[1] * decimated_power.shape[2]
    )
    padded = padded_2(series.astype(jnp.bfloat16), (("fft", 1),), HALF_WIDTH).astype(series.dtype)
    length = series.shape[1]
    window_sum = padded[:, 0:length]
    for offset in range(1, 2 * HALF_WIDTH + 1):
        window_sum = window_sum + padded[:, offset : offset + length]
    smoothed = window_sum / (2 * HALF_WIDTH + 1)
    return (spectrum_out, smoothed)


def solution(mesh):
    placed = (P("beam", "fft"), P("beam", "fft", None), P())
    return jax.shard_map(
        on_device,
        mesh=mesh,
        in_specs=placed,
        out_specs=(P("beam", "fft", None), P("beam", "fft")),
        check_vma=False,
    )
```

profile of v0, /device:TPU:16, one launch (start us, length us, event | category | flops | bytes accessed | tf_op | source)
XLA Modules:
  0.0 1084.0 jit_solution(8108217904448306539)
XLA Ops:
  2.5 11.9 %copy.194 = bf16[2,256,8192]{1,2,0:T(8,128)(2,1)} copy(bf16[2,256,8192]{2,1,0:T(8,128)(2,1)} %param.4) | data formatting | bytes 16777216 | tf_op args[1]
  14.4 11.5 %fusion.129 = (f32[1,1,256,64,128]{2,4,3,1,0:T(8,128)}, f32[1,1,256,64,128]{2,4,3,1,0:T(8,128)}) fusion(bf16[1,2,256,64,128]{2,4,3,1,0:T(8,128)(2,1)} %bitcast.212), kind=kLoop, calls=%fused_computation.287 | loop fusion | bytes 33554432 | tf_op jit(solution)/shard_map/slice | solution.py:77
  26.0 9.0 copy.240
  35.0 9.0 copy.241
  44.0 41.0 %fusion.57 = (bf16[1,256,64,128]{3,1,0,2:T(8,128)(2,1)S(1)}, bf16[1,256,64,128]{3,1,0,2:T(8,128)(2,1)S(1)}) fusion(f32[1,1,256,64,128]{4,2,3,1,0:T(8,128)} %copy.241, f32[1,1,256,64,128]{4,2,3,1,0:T(8,128)} %copy.240, f32[64,128]{1,0:T(8,128)S(1)} %fusion.97, s32[64,128]{1,0:T(8,128)S(1)} %iota_add_fusion.1, s32[256]{0:T(256)S(1)} %fusion.122, s32[]{:T(128)} %bitcast.60, ...), kind=kLoop, calls=%fused_computation.92 | loop fusion | flops 77594624 | bytes 25233412 | tf_op jit(solution)/shard_map/stack | solution.py:79
  85.0 7.0 fusion.47
  92.0 8.8 fusion.59
  100.8 6.3 pad_maximum_fusion.3
  107.2 12.2 %copy.200 = bf16[2,256,64,128]{3,2,0,1:T(8,128)(2,1)} copy(bf16[2,256,64,128]{1,3,2,0:T(8,128)(2,1)} %pad_maximum_fusion.3) | data formatting | bytes 16777216 | tf_op jit(solution)/shard_map/stack | solution.py:79
  119.4 5.8 fusion.48
  125.2 18.3 %copy.285 = f32[2,64,256,128]{3,2,1,0:T(8,128)S(1)} copy(f32[2,64,256,128]{3,1,2,0:T(8,128)S(1)} %fusion.48) | data formatting | bytes 33554432 | tf_op jit(solution)/shard_map/dimjy,iojx->domxy/dot_general | solution.py:83
  143.6 37.2 %subtract_convert_fusion.1 = (bf16[1,1,256,64,128]{4,2,3,1,0:T(8,128)(2,1)}, bf16[1,1,256,64,128]{4,2,3,1,0:T(8,128)(2,1)}) fusion(f32[1,2,256,64,128]{4,2,3,1,0:T(8,128)S(1)} %bitcast.213, s32[64,128]{1,0:T(8,128)S(1)} %iota_add_fusion, s32[256]{0:T(256)S(1)} %fusion.122), kind=kLoop, calls=%fused_computation.71 | loop fusion | flops 46137344 | bytes 25199616 | tf_op jit(solution)/shard_map/convert.9
  180.7 6.4 copy.202
  187.2 6.4 copy.203
  193.6 7.6 pad_maximum_fusion.4
  201.2 16.4 %copy.204 = bf16[1,2,256,8192]{2,1,0,3:T(2,128)(2,1)} copy(bf16[1,2,256,8192]{2,3,1,0:T(8,128)(2,1)} %pad_maximum_fusion.4) | data formatting | bytes 16777216 | tf_op jit(solution)/shard_map/stack | solution.py:79
  217.6 6.7 all-to-all-start.2
  224.3 12.7 %copy.286 = bf16[1,2,256,8192]{3,2,1,0:T(8,128)(2,1)} copy(bf16[1,2,256,8192]{3,1,2,0:T(2,128)(2,1)} %bitcast.228) | data formatting | bytes 16777216
  237.0 21.0 %copy.183 = bf16[2,256,8192]{1,0,2:T(2,128)(2,1)} copy(bf16[2,256,8192]{2,1,0:T(8,128)(2,1)} %bitcast.222) | data formatting | bytes 16777216 | tf_op jit(solution)/shard_map/reshape | solution.py:158
  258.0 148.7 %all-to-all-done.2 = bf16[1,2,256,8192]{2,1,0,3:T(2,128)(2,1)} async-done(((bf16[1,2,256,8192]{2,1,0,3:T(2,128)(2,1)}), bf16[1,2,256,8192]{2,1,0,3:T(2,128)(2,1)}, u32[]{:S(2)}, u32[]{:S(2)}) %all-to-all-start.2) | async-done | bytes 8388640 | tf_op jit(solution)/shard_map/all_to_all | solution.py:197
  414.0 7.9 copy.205
  421.8 11.9 %copy.206 = bf16[1,2,16,256,512]{4,3,2,1,0:T(8,128)(2,1)} copy(bf16[1,2,16,256,512]{3,4,2,1,0:T(8,128)(2,1)} %bitcast.219) | data formatting | bytes 16777216 | tf_op jit(solution)/shard_map/all_to_all | solution.py:197
  442.4 6.4 pad_maximum_fusion.5
  448.7 14.3 %fusion.14 = f32[2,32,128,512]{3,1,2,0:T(8,128)S(1)} fusion(bf16[2,32,128,512]{3,2,1,0:T(8,128)(2,1)} %pad_maximum_fusion.5, bf16[1,2,32,32]{2,3,1,0:T(8,128)(2,1)S(1)} %get-tuple-element.43, bf16[1,2,32,32]{2,3,1,0:T(8,128)(2,1)S(1)} %get-tuple-element.42), kind=kOutput, calls=%fused_computation.35 | convolution fusion | flops 545263616 | bytes 25174016 | tf_op jit(solution)/shard_map/dikyb,iokx->doxyb/dot_general | solution.py:83
  463.0 19.7 %copy.211 = f32[2,32,128,512]{3,2,1,0:T(8,128)} copy(f32[2,32,128,512]{3,1,2,0:T(8,128)S(1)} %fusion.14) | data formatting | bytes 33554432 | tf_op jit(solution)/shard_map/convert_element_type | solution.py:144
  482.7 9.6 fusion.15
  492.3 8.9 copy.212
  509.4 22.4 %reduce.2 = bf16[4096,32]{1,0:T(8,128)(2,1)S(1)} reduce(bf16[4096,1,32]{2,1,0:T(2,128)(2,1)S(1)} %bitcast.229, bf16[]{:T(256)} %broadcast.2052), dimensions={1}, to_apply=%bitcast.198.reduce_sub_computation | reduce | bytes 524290
  533.5 60.3 %all-to-all-done = bf16[2,256,8192]{1,0,2:T(2,128)(2,1)} async-done(((bf16[2,256,8192]{1,0,2:T(2,128)(2,1)}), bf16[2,256,8192]{1,0,2:T(2,128)(2,1)}, u32[]{:S(2)}, u32[]{:S(2)}) %all-to-all-start) | async-done | bytes 8388640 | tf_op jit(solution)/shard_map/all_to_all | solution.py:159
  598.7 7.9 copy.184
  606.5 11.9 %copy.185 = bf16[2,16,256,512]{3,2,1,0:T(8,128)(2,1)} copy(bf16[2,16,256,512]{2,3,1,0:T(8,128)(2,1)} %bitcast.220) | data formatting | bytes 16777216 | tf_op jit(solution)/shard_map/all_to_all | solution.py:159
  618.4 14.3 %fusion.36 = f32[1,2,32,128,512]{4,2,3,1,0:T(8,128)S(1)} fusion(bf16[2,32,128,512]{3,2,1,0:T(8,128)(2,1)} %bitcast.216, bf16[1,2,32,32]{2,3,0,1:T(8,128)(2,1)S(1)} %get-tuple-element.45, bf16[1,2,32,32]{2,3,0,1:T(8,128)(2,1)S(1)} %get-tuple-element.44), kind=kOutput, calls=%fused_computation.82 | convolution fusion | flops 536887296 | bytes 25174016 | tf_op jit(solution)/shard_map/dixyb,ioxk->dokyb/dot_general | solution.py:83
  636.9 6.3 pad_maximum_fusion
  643.2 13.8 %fusion.39 = f32[1,2,32,128,512]{4,3,2,1,0:T(8,128)S(1)} fusion(bf16[2,32,128,512]{3,1,2,0:T(8,128)(2,1)} %pad_maximum_fusion, bf16[1,2,128,128]{2,3,0,1:T(8,128)(2,1)S(1)} %get-tuple-element.37, bf16[1,2,128,128]{2,3,0,1:T(8,128)(2,1)S(1)} %get-tuple-element.36), kind=kOutput, calls=%fused_computation.83 | convolution fusion | flops 2147745792 | bytes 25296896 | tf_op jit(solution)/shard_map/dikyb,ioyq->dokqb/dot_general | solution.py:83
  657.0 36.5 %subtract_convert_fusion.5 = (bf16[1,1,32,128,512]{4,3,2,1,0:T(8,128)(2,1)S(1)}, bf16[1,1,32,128,512]{4,3,2,1,0:T(8,128)(2,1)S(1)}) fusion(f32[1,2,32,128,512]{4,3,2,1,0:T(8,128)S(1)} %fusion.39, s32[512]{0:T(512)S(1)} %iota_add_fusion.3, s32[32,128]{1,0:T(8,128)S(1)} %iota_add_fusion.2), kind=kLoop, calls=%fused_computation.79 | loop fusion | flops 46137344 | bytes 25184256 | tf_op jit(solution)/shard_map/convert.49
  693.5 31.1 %copy.190 = bf16[1,1,4096,512]{3,1,0,2:T(2,128)(2,1)S(1)} copy(bf16[1,1,4096,512]{3,2,1,0:T(8,128)(2,1)S(1)} %bitcast.224) | data formatting | bytes 8388608 | tf_op jit(solution)/shard_map/stack | solution.py:79
  724.6 31.1 %copy.191 = bf16[1,1,4096,512]{3,1,0,2:T(2,128)(2,1)S(1)} copy(bf16[1,1,4096,512]{3,2,1,0:T(8,128)(2,1)S(1)} %bitcast.223) | data formatting | bytes 8388608 | tf_op jit(solution)/shard_map/stack | solution.py:79
  755.7 20.3 %pad_maximum_fusion.1 = bf16[1,2,4096,512]{3,1,0,2:T(2,128)(2,1)} fusion(bf16[1,1,4096,512]{3,1,0,2:T(2,128)(2,1)S(1)} %copy.191, bf16[1,1,4096,512]{3,1,0,2:T(2,128)(2,1)S(1)} %copy.190), kind=kLoop, calls=%fused_computation.41 | loop fusion | flops 16777216 | bytes 16777216 | tf_op jit(solution)/shard_map/stack | solution.py:79
  776.0 6.2 all-to-all-start.1
  793.8 170.2 %collective-permute-done = bf16[1,16]{1,0:T(2,128)(2,1)S(1)} collective-permute-done((bf16[1,16]{1,0:T(2,128)(2,1)S(1)}, bf16[1,16]{1,0:T(2,128)(2,1)S(1)}, u32[]{:S(2)}, u32[]{:S(2)}) %collective-permute-start) | collective-permute-done | bytes 64 | tf_op jit(solution)/shard_map/ppermute | solution.py:25
  964.1 7.9 dynamic-update-slice.1
  972.9 36.0 %fusion.69 = f32[1,131072]{1,0:T(1,128)} fusion(f32[1,131104]{1,0:T(1,128)S(1)} %convert_element_type.400), kind=kLoop, calls=%fused_computation.105 | loop fusion | flops 4325376 | bytes 17825792 | tf_op jit(solution)/shard_map/div | solution.py:210
  1008.9 15.9 %copy.287 = bf16[1,2,16,256,512]{4,2,1,3,0:T(8,128)(2,1)} copy(bf16[1,2,16,256,512]{4,1,3,2,0:T(2,128)(2,1)} %bitcast.33) | data formatting | bytes 16777216 | tf_op jit(solution)/shard_map/all_to_all | solution.py:180
  1024.7 13.9 %reshape.1466 = bf16[2,256,64,128,1]{3,2,0,1,4:T(8,128)(2,1)} reshape(bf16[1,2,256,16,512]{4,3,1,2,0:T(8,128)(2,1)} %bitcast.221) | data formatting | bytes 16777216 | tf_op jit(solution)/shard_map/reshape.24
  1038.7 5.8 convolution_bitcast_fusion
  1048.6 6.4 pad_maximum_fusion.2
  1054.9 16.7 %bitcast_convert_fusion.1 = bf16[2,128,256,64]{2,1,3,0:T(8,128)(2,1)} fusion(bf16[2,256,64,128]{3,2,1,0:T(8,128)(2,1)} %pad_maximum_fusion.2, bf16[1,2,128,128]{2,3,0,1:T(8,128)(2,1)S(1)} %get-tuple-element.37, bf16[1,2,128,128]{2,3,0,1:T(8,128)(2,1)S(1)} %get-tuple-element.36), kind=kOutput, calls=%fused_computation.1 | convolution fusion | flops 2151940096 | bytes 16908288 | tf_op jit(solution)/shard_map/dimjy,ioyq->domjq/dot_general | solution.py:83
  1071.7 12.0 %copy.216 = bf16[2,256,8192]{2,1,0:T(8,128)(2,1)} copy(bf16[2,256,8192]{1,2,0:T(8,128)(2,1)} %bitcast.217) | data formatting | bytes 16777216
  (67 shorter events, 52.7 us)
Async XLA Ops:
  217.6 189.1 %all-to-all-start.2 = ((bf16[1,2,256,8192]{2,1,0,3:T(2,128)(2,1)}), bf16[1,2,256,8192]{2,1,0,3:T(2,128)(2,1)}, u32[]{:S(2)}, u32[]{:S(2)}) async-start(bf16[1,2,256,8192]{2,1,0,3:T(2,128)(2,1)} %copy.204), calls=%async_computation.2 | async-start | bytes 16777216 | tf_op jit(solution)/shard_map/all_to_all | solution.py:197
  406.7 187.1 %all-to-all-start = ((bf16[2,256,8192]{1,0,2:T(2,128)(2,1)}), bf16[2,256,8192]{1,0,2:T(2,128)(2,1)}, u32[]{:S(2)}, u32[]{:S(2)}) async-start(bf16[2,256,8192]{1,0,2:T(2,128)(2,1)} %copy.183), calls=%async_computation | async-start | bytes 16777216 | tf_op jit(solution)/shard_map/all_to_all | solution.py:159
  593.8 182.2 %all-to-all-start.3 = ((bf16[16,2,4096]{2,1,0:T(2,128)(2,1)}), bf16[16,2,4096]{2,1,0:T(2,128)(2,1)S(1)}, u32[]{:S(2)}, u32[]{:S(2)}) async-start(bf16[16,2,4096]{2,1,0:T(2,128)(2,1)} %reshape.1483), calls=%async_computation.3 | async-start | bytes 524288 | tf_op jit(solution)/shard_map/all_to_all | solution.py:199
  776.0 188.0 %copy-start = (bf16[1,131104]{1,0:T(2,128)(2,1)S(1)}, bf16[1,131104]{1,0:T(2,128)(2,1)}, u32[]{:S(2)}) copy-start(bf16[1,131104]{1,0:T(2,128)(2,1)} %custom-call) | copy-start | bytes 786628
  776.0 232.9 %all-to-all-start.1 = ((bf16[1,2,4096,512]{3,1,0,2:T(2,128)(2,1)}), bf16[1,2,4096,512]{3,1,0,2:T(2,128)(2,1)}, u32[]{:S(2)}, u32[]{:S(2)}) async-start(bf16[1,2,4096,512]{3,1,0,2:T(2,128)(2,1)} %pad_maximum_fusion.1), calls=%async_computation.1 | async-start | bytes 16777216 | tf_op jit(solution)/shard_map/all_to_all | solution.py:180
  787.3 176.7 %collective-permute-start = (bf16[1,16]{1,0:T(2,128)(2,1)S(1)}, bf16[1,16]{1,0:T(2,128)(2,1)S(1)}, u32[]{:S(2)}, u32[]{:S(2)}) collective-permute-start(bf16[1,16]{1,0:T(2,128)(2,1)S(1)} %get-tuple-element.33), channel_id=1, source_target_pairs={{0,1},{1,2},{2,3},{3,4},{4,5},{5,6},{6,7},{7,8},{8,9},{9,10},{10,1... | collective-permute-start | bytes 104 | tf_op jit(solution)/shard_map/ppermute | solution.py:25
  789.4 182.7 %collective-permute-start.1 = (bf16[1,16]{1,0:T(2,128)(2,1)S(1)}, bf16[1,16]{1,0:T(2,128)(2,1)S(1)}, u32[]{:S(2)}, u32[]{:S(2)}) collective-permute-start(bf16[1,16]{1,0:T(2,128)(2,1)S(1)} %get-tuple-element.32), channel_id=1, source_target_pairs={{1,0},{2,1},{3,2},{4,3},{5,4},{6,5},{7,6},{8,7},{9,8},{10,9},{11,1... | collective-permute-start | bytes 104 | tf_op jit(solution)/shard_map/ppermute | solution.py:28
  1038.7 5.8 copy-start.1
  1038.7 5.8 copy-start.2
where the time goes:
time: 1100 us; the launch traced here: 1080 us
  waiting for transfers between devices  379 us (34%)
  local copies, waits for them, and re-layouts  325 us (30%)
  other arithmetic  266 us (24%)
  matrix products  82.4 us (7%)
  starting transfers between devices  28.9 us (3%)
    ppermute x1, waiting for transfers between devices, padded_2(): lax.ppermute(lax.slice_in_dim(block, block.shape[dim] - width, None, axis...  170 us
    all_to_all x1, waiting for transfers between devices, on_device(): lax.all_to_all(front_part, 'fft', split_axis=3, concat_axis=2, tiled=True)  149 us
    another operation x11, other arithmetic, rotate(): return jnp.stack([real_part, imag_part], axis=1).astype(jnp.bfloat16)  115 us
    another operation x4, local copies, waits for them, and re-layouts, rotate(): return jnp.stack([real_part, imag_part], axis=1).astype(jnp.bfloat16)  90.7 us
    dot_general x8, matrix products, dft_section(): jnp.einsum(einsum_form, values, dft_table(length, direction), preferred_e...  82.4 us
    another operation x14, other arithmetic  75.7 us
    unnamed x17, local copies, waits for them, and re-layouts  66.2 us
    all_to_all x1, waiting for transfers between devices, on_device(): lax.all_to_all(values, 'fft', split_axis=2, concat_axis=1, tiled=True)  60.3 us
  transfers between devices with their start and end apart: 6, of which 3 were waited for; matrix products, arithmetic and copies ran while one was open for 35% of the time, Pallas kernels for 0%

commit v1 on v0

v1 whole, which is shorter than its diff:
```python
import math

import jax
import jax.numpy as jnp
from jax import lax
from jax.experimental import pallas as pl
from jax.experimental.pallas import tpu as pltpu
from jax.sharding import PartitionSpec as P

ROWS_OUTER = 32
ROWS_INNER = 128
COLS_OUTER = 64
COLS_INNER = 128
ROW_LENGTH = 4096
COLUMN_LENGTH = 8192
SEGMENT_SAMPLES = 33554432
DM_GRID = 64
DECIMATE_FACTOR = 16
HALF_WIDTH = 16
BLOCK_ROWS = 16
GROUP = 16
F32 = jnp.float32
BF16 = jnp.bfloat16


def dft_table(length, direction):
    positions = jnp.arange(length, dtype=jnp.int32)
    product = jnp.remainder(positions[:, None] * positions[None, :], length)
    radians = direction * 2.0 * math.pi / length * product.astype(F32)
    norm_scale = 1.0 / math.sqrt(length)
    cosine = jnp.cos(radians) * norm_scale
    sine_part = jnp.sin(radians) * norm_scale
    return jnp.stack([jnp.stack([cosine, sine_part]), jnp.stack([-sine_part, cosine])]).astype(BF16)


def right_table(length, direction):
    return dft_table(length, direction).transpose(0, 2, 1, 3).reshape(2 * length, 2 * length)


def left_table(length, direction):
    return dft_table(length, direction).transpose(1, 3, 0, 2).reshape(2 * length, 2 * length)


def phases(numer, modulus, direction=1):
    radians = direction * 2.0 * math.pi / modulus * jnp.remainder(numer, modulus).astype(F32)
    return jnp.stack([jnp.cos(radians), jnp.sin(radians)])


def row_frequency(row_pos):
    return row_pos // ROWS_INNER + ROWS_OUTER * (row_pos % ROWS_INNER)


def times(a, b):
    return a[0] * b[0] - a[1] * b[1], a[0] * b[1] + a[1] * b[0]


def dot(a, b):
    return jnp.dot(a, b, preferred_element_type=F32)


def stacked(ref, place):
    return jnp.concatenate([ref[0, place, :].astype(BF16), ref[1, place, :].astype(BF16)], axis=0)


def keep(ref, place, pair):
    ref[0, place, :] = pair[0]
    ref[1, place, :] = pair[1]


def pieces(row_local):
    step = min(row_local, ROWS_INNER)
    return [
        (start, start // row_local, start % row_local, step)
        for start in range(0, ROW_LENGTH, step)
    ]


def front_kernel(spec, a_tab, q_tab, c_tab, cy_tab, x_tab, y_tab, e_in, e_out, out, first, second):
    rows = BLOCK_ROWS
    q = (q_tab[0], q_tab[1])
    for c in range(COLS_OUTER):
        cols = slice(c * COLS_INNER, (c + 1) * COLS_INNER)
        turn = times((a_tab[0, :, c : c + 1], a_tab[1, :, c : c + 1]), q)
        turn = times(turn, (c_tab[0, c : c + 1, :], c_tab[1, c : c + 1, :]))
        value = times((spec[0, :, cols].astype(F32), spec[1, :, cols].astype(F32)), turn)
        both = jnp.concatenate([value[0].astype(BF16), value[1].astype(BF16)], axis=1)
        mixed = dot(both, e_in[...])
        w1 = times(
            (mixed[:, :COLS_INNER], mixed[:, COLS_INNER:]),
            (cy_tab[0, c : c + 1, :], cy_tab[1, c : c + 1, :]),
        )
        keep(first, slice(c * rows, (c + 1) * rows), w1)
    for m in range(rows):
        mixed = dot(e_out[...], stacked(first, pl.ds(m, COLS_OUTER, stride=rows)))
        turn = times(
            (x_tab[0, 0, :, m : m + 1], x_tab[1, 0, :, m : m + 1]),
            (y_tab[0, m : m + 1, :], y_tab[1, m : m + 1, :]),
        )
        w2 = times((mixed[:COLS_OUTER], mixed[COLS_OUTER:]), turn)
        keep(second, slice(m * COLS_OUTER, (m + 1) * COLS_OUTER), w2)
    wide = out.shape[3] // COLS_INNER
    for x in range(COLS_OUTER):
        place = (x % wide) * COLS_INNER
        for part in range(2):
            out[x // wide, part, :, place : place + COLS_INNER] = second[
                part, pl.ds(x, rows, stride=COLS_OUTER), :
            ].astype(BF16)


def back_kernel(word, cy_tab, e_in, e_out, out, first, second):
    rows = BLOCK_ROWS
    wide = word.shape[3] // COLS_INNER
    for x in range(COLS_OUTER):
        place = (x % wide) * COLS_INNER
        for part in range(2):
            first[part, x * rows : (x + 1) * rows, :] = word[
                x // wide, part, :, place : place + COLS_INNER
            ].astype(F32)
    cy = (cy_tab[0], cy_tab[1])
    for m in range(rows):
        mixed = dot(e_in[...], stacked(first, pl.ds(m, COLS_OUTER, stride=rows)))
        v1 = times((mixed[:COLS_OUTER], mixed[COLS_OUTER:]), cy)
        both = jnp.concatenate([v1[0].astype(BF16), v1[1].astype(BF16)], axis=1)
        mixed = dot(both, e_out[...])
        keep(
            second,
            slice(m * COLS_OUTER, (m + 1) * COLS_OUTER),
            (mixed[:, :COLS_INNER], mixed[:, COLS_INNER:]),
        )
    for c in range(COLS_OUTER):
        cols = slice(c * COLS_INNER, (c + 1) * COLS_INNER)
        for part in range(2):
            out[part, :, cols] = second[part, pl.ds(c, rows, stride=COLS_OUTER), :].astype(BF16)


def rows_kernel(word, pn_tab, col_tab, py_tab, qy_tab, e_in, e_out, out, first, second):
    outer, inner = ROWS_OUTER, ROWS_INNER
    row_local = word.shape[2]
    for start, shard, local, step in pieces(row_local):
        for part in range(2):
            first[part, start : start + step, :] = word[
                shard, part, local : local + step, :
            ].astype(F32)
    for n in range(inner):
        mixed = dot(e_in[...], stacked(first, pl.ds(n, outer, stride=inner)))
        u1 = times(
            (mixed[:outer], mixed[outer:]), (pn_tab[0, :, n : n + 1], pn_tab[1, :, n : n + 1])
        )
        keep(second, slice(n * outer, (n + 1) * outer), u1)
    qy = (qy_tab[0], qy_tab[1])
    for p in range(outer):
        mixed = dot(e_out[...], stacked(second, pl.ds(p, inner, stride=outer)))
        turn = times(
            (col_tab[0, 0, :, p : p + 1], col_tab[1, 0, :, p : p + 1]),
            (py_tab[0, p : p + 1, :], py_tab[1, p : p + 1, :]),
        )
        u2 = times((mixed[:inner], mixed[inner:]), times(turn, qy))
        for start, shard, local, step in pieces(row_local):
            if start // inner == p:
                low = start % inner
                for part in range(2):
                    out[shard, part, local : local + step, :] = u2[part][low : low + step].astype(
                        BF16
                    )


def detect_kernel(word, np_tab, e_in, e_out, sum_tab, out, first):
    outer, inner = ROWS_OUTER, ROWS_INNER
    row_local = word.shape[2]
    for p in range(outer):
        held = [
            [
                word[shard, part, local : local + step, :]
                for start, shard, local, step in pieces(row_local)
                if start // inner == p
            ]
            for part in range(2)
        ]
        mixed = dot(e_in[...], jnp.concatenate(held[0] + held[1], axis=0))
        w3 = times(
            (mixed[:inner], mixed[inner:]), (np_tab[0, :, p : p + 1], np_tab[1, :, p : p + 1])
        )
        keep(first, slice(p * inner, (p + 1) * inner), w3)

    def gather(group, carry):
        total = jnp.zeros((outer, COLS_INNER), F32)
        for r in range(GROUP):
            mixed = dot(e_out[...], stacked(first, pl.ds(group * GROUP + r, outer, stride=inner)))
            signal = mixed.astype(BF16).astype(F32)
            power = signal[:outer] * signal[:outer] + signal[outer:] * signal[outer:]
            high = power.astype(BF16)
            low = (power - high.astype(F32)).astype(BF16)
            total = total + dot(high, sum_tab[r]) + dot(low, sum_tab[r])
        out[0, group] = total
        return carry

    lax.fori_loop(0, inner // GROUP, gather, 0)


def params():
    return pltpu.CompilerParams(
        dimension_semantics=("arbitrary",), vmem_limit_bytes=56 * 1024 * 1024
    )


def cost():
    return pl.CostEstimate(flops=12_000_000_000, bytes_accessed=40_000_000, transcendentals=0)


def whole_spec(array):
    zeros = (0,) * array.ndim
    return pl.BlockSpec(array.shape, lambda i: zeros)


def swap(values):
    return lax.all_to_all(values, "fft", split_axis=0, concat_axis=0, tiled=True)


def column_phases():
    c = jnp.arange(COLS_OUTER, dtype=jnp.int32)[:, None]
    y = jnp.arange(COLS_INNER, dtype=jnp.int32)[None, :]
    return c, y


def front(spectrum, grid_step, freq_row, shards):
    row_local = spectrum.shape[1]
    rows = BLOCK_ROWS
    blocks = row_local // rows
    c, y = column_phases()
    k = freq_row[:, None]
    cross_mod = 2 * DM_GRID * COLUMN_LENGTH
    square = (grid_step * (k * k)).astype(F32) / (4.0 * DM_GRID * ROW_LENGTH * COLUMN_LENGTH)
    cross = jnp.remainder(grid_step * (k * c.T), cross_mod).astype(F32) / cross_mod
    radians = 2.0 * math.pi * (square + cross)
    a_tab = jnp.stack([jnp.cos(radians), jnp.sin(radians)])
    q_tab = phases(grid_step * (k * y), cross_mod // COLS_OUTER)
    square_mod = 4 * DM_GRID * COLUMN_LENGTH // ROW_LENGTH
    column = c + COLS_OUTER * y
    c_tab = phases(grid_step * jnp.remainder(column * column, square_mod), square_mod)
    cy_tab = phases(c * y, COLUMN_LENGTH)
    x_tab = phases(freq_row.reshape(blocks, 1, rows) * c[None], SEGMENT_SAMPLES // COLS_INNER)
    y_tab = phases(k * y, SEGMENT_SAMPLES)
    e_in, e_out = right_table(COLS_INNER, 1), left_table(COLS_OUTER, 1)
    row_block = lambda width: pl.BlockSpec((2, rows, width), lambda i: (0, i, 0))
    return pl.pallas_call(
        front_kernel,
        grid=(blocks,),
        in_specs=[
            row_block(COLUMN_LENGTH),
            row_block(COLS_OUTER),
            row_block(COLS_INNER),
            whole_spec(c_tab),
            whole_spec(cy_tab),
            pl.BlockSpec((2, 1, COLS_OUTER, rows), lambda i: (0, i, 0, 0)),
            row_block(COLS_INNER),
            whole_spec(e_in),
            whole_spec(e_out),
        ],
        out_specs=pl.BlockSpec((shards, 2, rows, COLUMN_LENGTH // shards), lambda i: (0, 0, i, 0)),
        out_shape=jax.ShapeDtypeStruct((shards, 2, row_local, COLUMN_LENGTH // shards), BF16),
        scratch_shapes=[pltpu.VMEM((2, rows * COLS_OUTER, COLS_INNER), F32)] * 2,
        compiler_params=params(),
        cost_estimate=cost(),
        name="front",
    )(spectrum, a_tab, q_tab, c_tab, cy_tab, x_tab, y_tab, e_in, e_out)


def back(words):
    shards, _, row_local, width = words.shape
    rows = BLOCK_ROWS
    c, y = column_phases()
    cy_tab = phases(c * y, COLUMN_LENGTH, -1)
    e_in, e_out = left_table(COLS_OUTER, -1), right_table(COLS_INNER, -1)
    return pl.pallas_call(
        back_kernel,
        grid=(row_local // rows,),
        in_specs=[
            pl.BlockSpec((shards, 2, rows, width), lambda i: (0, 0, i, 0)),
            whole_spec(cy_tab),
            whole_spec(e_in),
            whole_spec(e_out),
        ],
        out_specs=pl.BlockSpec((2, rows, COLUMN_LENGTH), lambda i: (0, i, 0)),
        out_shape=jax.ShapeDtypeStruct((2, row_local, COLUMN_LENGTH), BF16),
        scratch_shapes=[pltpu.VMEM((2, rows * COLS_OUTER, COLS_INNER), F32)] * 2,
        compiler_params=params(),
        cost_estimate=cost(),
        name="back",
    )(words, cy_tab, e_in, e_out)


def row_section(words, device_index):
    shards, _, row_local, width = words.shape
    tiles = width // COLS_INNER
    p = jnp.arange(ROWS_OUTER, dtype=jnp.int32)
    q = jnp.arange(ROWS_INNER, dtype=jnp.int32)
    y = jnp.arange(COLS_INNER, dtype=jnp.int32)
    pn_tab = phases(p[:, None] * q[None, :], ROW_LENGTH, -1)
    tile = device_index * tiles + jnp.arange(tiles, dtype=jnp.int32)
    k = p[None, :] + ROWS_OUTER * q[:, None]
    col_tab = phases(tile[:, None, None] * k[None], SEGMENT_SAMPLES // COLS_INNER, -1)
    py_tab = phases(p[:, None] * y[None, :], SEGMENT_SAMPLES, -1)
    qy_tab = phases(q[:, None] * y[None, :], SEGMENT_SAMPLES // ROWS_OUTER, -1)
    e_in, e_out = left_table(ROWS_OUTER, -1), left_table(ROWS_INNER, -1)
    block = pl.BlockSpec((shards, 2, row_local, COLS_INNER), lambda i: (0, 0, 0, i))
    return pl.pallas_call(
        rows_kernel,
        grid=(tiles,),
        in_specs=[
            block,
            whole_spec(pn_tab),
            pl.BlockSpec((2, 1, ROWS_INNER, ROWS_OUTER), lambda i: (0, i, 0, 0)),
            whole_spec(py_tab),
            whole_spec(qy_tab),
            whole_spec(e_in),
            whole_spec(e_out),
        ],
        out_specs=block,
        out_shape=jax.ShapeDtypeStruct(words.shape, BF16),
        scratch_shapes=[pltpu.VMEM((2, ROW_LENGTH, COLS_INNER), F32)] * 2,
        compiler_params=params(),
        cost_estimate=cost(),
        name="row_section",
    )(words, pn_tab, col_tab, py_tab, qy_tab, e_in, e_out)


def detect(words):
    shards, _, row_local, width = words.shape
    tiles = width // COLS_INNER
    p = jnp.arange(ROWS_OUTER, dtype=jnp.int32)
    n = jnp.arange(ROWS_INNER, dtype=jnp.int32)
    np_tab = phases(n[:, None] * p[None, :], ROW_LENGTH)
    e_in, e_out = left_table(ROWS_INNER, 1), left_table(ROWS_OUTER, 1)
    lane = jnp.arange(COLS_INNER, dtype=jnp.int32)
    short = COLS_INNER // DECIMATE_FACTOR
    slot = jnp.arange(GROUP, dtype=jnp.int32)[:, None] * short + lane[None, :] // DECIMATE_FACTOR
    sum_tab = ((slot[:, :, None] == lane[None, None, :]) / DECIMATE_FACTOR).astype(BF16)
    groups = ROWS_INNER // GROUP
    power = pl.pallas_call(
        detect_kernel,
        grid=(tiles,),
        in_specs=[
            pl.BlockSpec((shards, 2, row_local, COLS_INNER), lambda i: (0, 0, 0, i)),
            whole_spec(np_tab),
            whole_spec(e_in),
            whole_spec(e_out),
            whole_spec(sum_tab),
        ],
        out_specs=pl.BlockSpec((1, groups, ROWS_OUTER, COLS_INNER), lambda i: (i, 0, 0, 0)),
        out_shape=jax.ShapeDtypeStruct((tiles, groups, ROWS_OUTER, COLS_INNER), F32),
        scratch_shapes=[pltpu.VMEM((2, ROW_LENGTH, COLS_INNER), F32)],
        compiler_params=params(),
        cost_estimate=cost(),
        name="detect",
    )(words, np_tab, e_in, e_out, sum_tab)
    power = power.astype(BF16).reshape(tiles, groups, ROWS_OUTER, GROUP, short)
    return power.transpose(2, 1, 3, 0, 4).reshape(ROW_LENGTH, tiles * short)


def smooth(series):
    count = lax.axis_size("fft")
    forward = [(i, i + 1) for i in range(count - 1)]
    backward = [(target, source) for source, target in forward]
    low = lax.ppermute(series[-HALF_WIDTH:], "fft", forward)
    high = lax.ppermute(series[:HALF_WIDTH], "fft", backward)
    length = series.shape[0]
    frames = series.reshape(length // 128, 128)
    before = jnp.concatenate([low[None], frames[:-1, -HALF_WIDTH:]], axis=0)
    after = jnp.concatenate([frames[1:, :HALF_WIDTH], high[None]], axis=0)
    frames = jnp.concatenate([before, frames, after], axis=1)
    source = jnp.arange(128 + 2 * HALF_WIDTH, dtype=jnp.int32)[:, None]
    target = jnp.arange(128, dtype=jnp.int32)[None, :]
    band = ((source >= target) & (source <= target + 2 * HALF_WIDTH)).astype(BF16)
    return (dot(frames, band) / (2 * HALF_WIDTH + 1)).reshape(length)


def on_device(baseband, spectrum_in, dm_index):
    device_index = lax.axis_index("fft")
    shards = lax.axis_size("fft")
    row_local = spectrum_in.shape[1]
    width = COLUMN_LENGTH // shards
    word = baseband.reshape(2, row_local, shards, width).transpose(2, 0, 1, 3)
    word, spectrum_in = lax.optimization_barrier((word, spectrum_in))
    time_rows = swap(word)
    grid_steps = dm_index + 1
    row_pos = device_index * row_local + jnp.arange(row_local, dtype=jnp.int32)
    freq_row = row_frequency(row_pos)
    trials = dm_index.shape[0]
    fronts = [front(spectrum_in, grid_steps[t], freq_row, shards) for t in range(trials)]
    time_rows, *fronts = lax.optimization_barrier((time_rows, *fronts))
    moved = [swap(item) for item in fronts]
    partial = row_section(time_rows, device_index)
    partial, *moved = lax.optimization_barrier((partial, *moved))
    partial = swap(partial)
    powers = [detect(item) for item in moved]
    partial, *powers = lax.optimization_barrier((partial, *powers))
    results = []
    for power in powers:
        power = swap(power.reshape(shards, row_local, width // DECIMATE_FACTOR))
        results.append(smooth(power.transpose(1, 0, 2).reshape(-1)))
    return back(partial), jnp.stack(results)


def solution(mesh):
    placed = (P("beam", "fft"), P("beam", "fft", None), P())
    return jax.shard_map(
        on_device,
        mesh=mesh,
        in_specs=placed,
        out_specs=(P("beam", "fft", None), P("beam", "fft")),
        check_vma=False,
    )
```

time: 1100 us -> 638 us (0.58); the launches traced: 1080 us -> 635 us
  local copies, waits for them, and re-layouts: 325 us -> 37.4 us
  other arithmetic: 266 us -> 13.6 us
  Pallas kernels: 0 us -> 170 us
  matrix products: 82.4 us -> 1.26 us
    another operation x25 -> x23, other arithmetic: 191 us -> 7.42 us  [the longest x10 4.65 us: phases(): return jnp.stack([jnp.cos(radians), jnp.sin(radians)])]
    all_to_all x4, waiting for transfers between devices: 209 us -> 382 us  [swap(): lax.all_to_all(values, 'fft', split_axis=0, concat_axis=0, tiled=True)]
    pallas_call x0 -> x4, Pallas kernels: none -> 170 us  [the longest x1 55.3 us: detect(): pl.pallas_call(detect_kernel, grid=(tiles,), in_specs=[pl.BlockSpec((shar...]
    ppermute x2, waiting for transfers between devices: 170 us -> 1.27 us  [the longest x1 1.26 us: smooth(): high = lax.ppermute(series[:HALF_WIDTH], 'fft', backward)]
    another operation x7 -> x4, local copies, waits for them, and re-layouts: 117 us -> 3.57 us  [the longest x3 3.07 us: phases(): return jnp.stack([jnp.cos(radians), jnp.sin(radians)])]
    dot_general x8 -> x1, matrix products: 82.4 us -> 1.26 us  [dot(): return jnp.dot(a, b, preferred_element_type=F32)]
    all_to_all x8 -> x0, local copies, waits for them, and re-layouts: 59 us -> none  [the longest x2 19.7 us: on_device(): lax.all_to_all(front_part, 'fft', split_axis=3, concat_axis=2, tiled=True)]
    unnamed x17 -> x5, local copies, waits for them, and re-layouts: 66.2 us -> 10.8 us
  transfers between devices with their start and end apart: 6 -> 6, of which waited for: 3 -> 4; matrix products, arithmetic and copies ran while one was open for 35% -> 5% of each run, Pallas kernels for 0% -> 27%
where the time goes in v1:
time: 638 us; the launch traced here: 635 us
  waiting for transfers between devices  384 us (60%)
  Pallas kernels  170 us (27%)
  local copies, waits for them, and re-layouts  37.4 us (6%)
  starting transfers between devices  27 us (4%)
  other arithmetic  13.6 us (2%)
    all_to_all x4, waiting for transfers between devices, swap(): lax.all_to_all(values, 'fft', split_axis=0, concat_axis=0, tiled=True)  382 us
    pallas_call x1, Pallas kernels, detect(): pl.pallas_call(detect_kernel, grid=(tiles,), in_specs=[pl.BlockSpec((shar...  55.3 us
    pallas_call x1, Pallas kernels, front(): pl.pallas_call(front_kernel, grid=(blocks,), in_specs=[row_block(COLUMN_L...  44.8 us
    pallas_call x1, Pallas kernels, back(): pl.pallas_call(back_kernel, grid=(row_local // rows,), in_specs=[pl.Block...  35.4 us
    pallas_call x1, Pallas kernels, row_section(): pl.pallas_call(rows_kernel, grid=(tiles,), in_specs=[block, whole_spec(pn...  35 us
    all_to_all x4, starting transfers between devices, swap(): lax.all_to_all(values, 'fft', split_axis=0, concat_axis=0, tiled=True)  20.6 us
  transfers between devices with their start and end apart: 6, of which 4 were waited for; matrix products, arithmetic and copies ran while one was open for 5% of the time, Pallas kernels for 27%

profile of v1, /device:TPU:16, one launch (start us, length us, event | category | flops | bytes accessed | tf_op | source)
XLA Modules:
  0.0 635.1 jit_solution(2848284863401580107)
XLA Ops:
  0.6 8.1 %copy.65 = bf16[1,2,4096,512]{3,2,1,0:T(8,128)(2,1)} copy(bf16[1,2,4096,512]{3,1,2,0:T(2,128)(2,1)} %bitcast.84) | data formatting | bytes 16777216
  8.8 11.4 %copy.76 = bf16[2,256,16,512]{3,1,0,2:T(8,128)(2,1)} copy(bf16[2,256,16,512]{3,2,1,0:T(8,128)(2,1)} %bitcast.83) | data formatting | bytes 16777216 | tf_op jit(solution)/shard_map/reshape | solution.py:382
  20.1 6.2 all-to-all-start
  27.0 0.6 fusion.49
  27.6 1.3 copy.50.x_tab
  29.7 0.7 copy.81
  30.8 0.7 reshape.1505.e_out
  31.9 0.6 pad_maximum_fusion.8.c_tab
  32.5 0.6 pad_maximum_fusion.9.cy_tab
  33.1 0.6 fusion.53
  33.8 0.7 pad_maximum_fusion.a_tab
  34.5 1.1 fusion.51
  35.6 0.9 pad_maximum_fusion.1
  36.4 44.8 %front.1 = bf16[16,2,256,512]{3,2,1,0:T(8,128)(2,1)} custom-call(bf16[2,256,8192]{2,1,0:T(8,128)(2,1)} %spec, f32[2,256,64]{2,1,0:T(8,128)} %pad_maximum_fusion.a_tab, f32[2,256,128]{2,1,0:T(8,128)} %get-tuple-element.50.q_tab, f32[2,64,128]{2,1,0:T(8,128)} %pad_maximum_fusion.8.c_tab, f32[2,64,128]{2,1,0:T(8,128)} %pad_maximum_fusion.9.cy_tab, ...), custom_call_target="tpu_custom_call" | custom-call | flops 12000000000 | bytes 40000000 | tf_op jit(solution)/shard_map/front/pallas_call | solution.py:245
  81.2 127.6 %all-to-all-done.word = bf16[16,2,256,512]{3,2,1,0:T(8,128)(2,1)} async-done(((bf16[16,2,256,512]{3,2,1,0:T(8,128)(2,1)}), bf16[16,2,256,512]{3,2,1,0:T(8,128)(2,1)}, u32[]{:S(2)}, u32[]{:S(2)}) %all-to-all-start) | async-done | bytes 8388640 | tf_op jit(solution)/shard_map/all_to_all | solution.py:216
  208.9 4.9 all-to-all-start.1
  214.5 0.7 copy.80
  215.5 0.7 reshape.1506.e_in
  216.5 1.0 copy.53.col_tab
  217.7 0.6 pad_maximum_fusion.11.pn_tab
  218.3 0.6 pad_maximum_fusion.12.py_tab
  219.2 0.7 pad_maximum_fusion.6.qy_tab
  219.9 35.0 %row_section.1 = bf16[16,2,256,512]{3,2,1,0:T(8,128)(2,1)} custom-call(bf16[16,2,256,512]{3,2,1,0:T(8,128)(2,1)} %all-to-all-done.word, f32[2,32,128]{2,1,0:T(8,128)} %pad_maximum_fusion.11.pn_tab, f32[2,4,128,32]{3,2,1,0:T(8,128)} %copy.53.col_tab, f32[2,32,128]{2,1,0:T(8,128)} %pad_maximum_fusion.12.py_tab, f32[2,128,128]{2,1,0:T(8,128)} %pad_maximum_fusion.6.qy_tab, ...), custom_call_target="tpu_custom_call" | custom-call | flops 12000000000 | bytes 40000000 | tf_op jit(solution)/shard_map/row_section/pallas_call | solution.py:306
  254.9 141.1 %all-to-all-done.1.word = bf16[16,2,256,512]{3,2,1,0:T(8,128)(2,1)} async-done(((bf16[16,2,256,512]{3,2,1,0:T(8,128)(2,1)}), bf16[16,2,256,512]{3,2,1,0:T(8,128)(2,1)}, u32[]{:S(2)}, u32[]{:S(2)}) %all-to-all-start.1) | async-done | bytes 8388640 | tf_op jit(solution)/shard_map/all_to_all | solution.py:216
  396.0 4.9 all-to-all-start.2
  401.0 0.7 copy.79
  402.0 0.7 reshape.1509.e_out
  402.8 0.7 copy.56.np_tab
  403.7 0.7 copy.78
  404.8 0.7 reshape.1512.e_in
  405.7 0.6 pad_maximum_fusion.10.cy_tab
  406.4 1.1 select_convert_fusion.sum_tab
  407.5 55.3 %detect.1 = f32[4,8,32,128]{3,2,1,0:T(8,128)} custom-call(bf16[16,2,256,512]{3,2,1,0:T(8,128)(2,1)} %all-to-all-done.1.word, f32[2,128,32]{2,1,0:T(8,128)} %copy.56.np_tab, bf16[256,256]{1,0:T(8,128)(2,1)} %bitcast.92, bf16[64,64]{1,0:T(8,128)(2,1)} %reshape.1509.e_out, bf16[16,128,128]{2,1,0:T(8,128)(2,1)} %select_convert_fusion.sum_tab), custom_call_target="tpu_custom_call" | custom-call | flops 12000000000 | bytes 40000000 | tf_op jit(solution)/shard_map/detect/pallas_call | solution.py:339
  462.8 1.1 convert_element_type.354
  463.9 0.5 copy.57
  464.4 1.5 copy.58
  465.9 3.6 reshape.1511
  469.5 113.7 %all-to-all-done.2.word = bf16[16,2,256,512]{3,2,1,0:T(8,128)(2,1)} async-done(((bf16[16,2,256,512]{3,2,1,0:T(8,128)(2,1)}), bf16[16,2,256,512]{3,2,1,0:T(8,128)(2,1)}, u32[]{:S(2)}, u32[]{:S(2)}) %all-to-all-start.2) | async-done | bytes 8388640 | tf_op jit(solution)/shard_map/all_to_all | solution.py:216
  583.1 0.7 copy.77
  583.8 4.6 all-to-all-start.3
  588.4 35.4 %back.1 = bf16[2,256,8192]{2,1,0:T(8,128)(2,1)} custom-call(bf16[16,2,256,512]{3,2,1,0:T(8,128)(2,1)} %all-to-all-done.2.word, f32[2,64,128]{2,1,0:T(8,128)} %pad_maximum_fusion.10.cy_tab, bf16[128,128]{1,0:T(8,128)(2,1)} %reshape.1512.e_in, bf16[256,256]{1,0:T(8,128)(2,1)} %bitcast.94), custom_call_target="tpu_custom_call" | custom-call | flops 12000000000 | bytes 40000000 | tf_op jit(solution)/shard_map/back/pallas_call | solution.py:274
  623.9 0.9 copy.62
  624.8 0.5 reshape_reshape.3
  625.3 0.5 reshape.1515
  626.1 2.0 collective-permute-start
  628.1 4.4 collective-permute-start.1
  632.6 1.3 collective-permute-done.1
  633.8 1.3 convolution_multiply_fusion
  (58 shorter events, 4.9 us)
Async XLA Ops:
  20.1 188.7 %all-to-all-start = ((bf16[16,2,256,512]{3,2,1,0:T(8,128)(2,1)}), bf16[16,2,256,512]{3,2,1,0:T(8,128)(2,1)}, u32[]{:S(2)}, u32[]{:S(2)}) async-start(bf16[16,2,256,512]{3,2,1,0:T(8,128)(2,1)} %bitcast.82), calls=%async_computation | async-start | bytes 16777216 | tf_op jit(solution)/shard_map/all_to_all | solution.py:216
  208.9 187.1 %all-to-all-start.1 = ((bf16[16,2,256,512]{3,2,1,0:T(8,128)(2,1)}), bf16[16,2,256,512]{3,2,1,0:T(8,128)(2,1)}, u32[]{:S(2)}, u32[]{:S(2)}) async-start(bf16[16,2,256,512]{3,2,1,0:T(8,128)(2,1)} %front.1), calls=%async_computation.1 | async-start | bytes 16777216 | tf_op jit(solution)/shard_map/all_to_all | solution.py:216
  396.0 187.1 %all-to-all-start.2 = ((bf16[16,2,256,512]{3,2,1,0:T(8,128)(2,1)}), bf16[16,2,256,512]{3,2,1,0:T(8,128)(2,1)}, u32[]{:S(2)}, u32[]{:S(2)}) async-start(bf16[16,2,256,512]{3,2,1,0:T(8,128)(2,1)} %row_section.1), calls=%async_computation.2 | async-start | bytes 16777216 | tf_op jit(solution)/shard_map/all_to_all | solution.py:216
  583.8 40.0 %all-to-all-start.3 = ((bf16[16,256,32]{1,2,0:T(8,128)(2,1)}), bf16[16,256,32]{1,2,0:T(8,128)(2,1)S(1)}, u32[]{:S(2)}, u32[]{:S(2)}) async-start(bf16[16,256,32]{1,2,0:T(8,128)(2,1)} %bitcast.77), calls=%async_computation.3 | async-start | bytes 524288 | tf_op jit(solution)/shard_map/all_to_all | solution.py:216
  626.1 6.5 %collective-permute-start = (bf16[16]{0:T(256)(128)(2,1)S(1)}, bf16[16]{0:T(256)(128)(2,1)S(1)}, u32[]{:S(2)}, u32[]{:S(2)}) collective-permute-start(bf16[16]{0:T(256)(128)(2,1)S(1)} %get-tuple-element.18), channel_id=1, source_target_pairs={{0,1},{1,2},{2,3},{3,4},{4,5},{5,6},{6,7},{7,8},{8,9},{9,10},{10,1... | collective-permute-start | bytes 104 | tf_op jit(solution)/shard_map/ppermute | solution.py:364
  628.1 5.7 collective-permute-start.1
